TPU v7x, 32 devices: a whole 2x2x4 slice. The times are simulated.
32 devices in a mesh: group: 2 (over x), expert: 16 (over z, y, core).
Axes of the slice: x: 2, y: 2, z: 4, core: 2. Of those that a mesh axis runs over, the one named last changes fastest.
Arguments:
- query: bfloat16 [32, 2048], P(('group', 'expert')), parts along dimension 0, may hold values from -600 to 600
- key_new: bfloat16 [32, 2048], P(('group', 'expert')), parts along dimension 0, may hold values from -6 to 6
- value_new: bfloat16 [32, 2048], P(('group', 'expert')), parts along dimension 0, may hold values from -6 to 6
- key_cache: bfloat16 [32, 256, 2048], P(('group', 'expert')), parts along dimension 0, may hold values from -6 to 6
- value_cache: bfloat16 [32, 256, 2048], P(('group', 'expert')), parts along dimension 0, may hold values from -6 to 6
- lengths: int32 [32], P(('group', 'expert')), parts along dimension 0, may hold values from 1 to 256
- hidden: bfloat16 [32, 2048], P(('group', 'expert')), parts along dimension 0, may hold values from -6 to 6
- routes: int32 [32], P('group'), parts along dimension 0, may hold values from 0 to 31, as said below
- w_out: bfloat16 [2048, 2048], P(None, 'expert'), may hold values from -0.125 to 0.125
- ln_gain: bfloat16 [2048], replicated, may hold values from 0.099609375 to 1.8984375
- router: bfloat16 [2048, 32], replicated, may hold values from -0.125 to 0.125
- shared_up: bfloat16 [2048, 8192], P(None, 'expert'), may hold values from -0.125 to 0.125
- shared_down: bfloat16 [8192, 2048], P('expert'), may hold values from -0.0625 to 0.0625
- expert_up: bfloat16 [2048, 131072], P(None, 'expert'), may hold values from -0.125 to 0.125
- expert_down: bfloat16 [131072, 2048], P('expert'), may hold values from -0.09375 to 0.09375
Outputs:
- layer_out: bfloat16 [32, 2048], P(('group', 'expert')), parts along dimension 0
There are 2 independent parts, one for each index of `group`. A program takes and returns all parts, laid end to end along the dimension named above; an argument that names none is the same for every part. Nothing has to cross between parts.
Inputs may be any that keep to these rules, and one draw needn't show every extreme that they name: `routes`: no expert is named by more than 2 tokens of the group, and in every draw some expert is named by exactly 2.
All inputs are finite; a program needn't handle non-finite values.
Results may differ from a plain program's by a relative error of at most 0.0085.
Values may be sent and summed in bfloat16 or wider, within the bound.
A program may use at most 128 MiB of HBM per device.

v0:
```python
import functools
import math

import jax
import jax.numpy as jnp
from jax import lax
from jax.experimental import pallas as pl
from jax.experimental.pallas import tpu as pltpu
from jax.sharding import PartitionSpec as P

HEADS = 16
HEAD_DIM = 128
FF = 4096
EXPERTS = 32
CHUNK = 512
BLOCK = 512
MAX_SLOTS = 26
EARLY = 3
PRIORITY = 1
TOGETHER = 4
JOINT = 1
GROUP_COLS = 1024
MESH = pl.DeviceIdType.MESH
F32 = jnp.float32
BF16 = jnp.bfloat16


def gelu(v):
    return 0.5 * v * (1.0 + jnp.tanh(math.sqrt(2.0 / math.pi) * (v + 0.044715 * (v * v * v))))


def kernel(
    n,
    slots,
    lengths_hbm,
    routes_hbm,
    query_hbm,
    key_new_hbm,
    value_new_hbm,
    hidden_hbm,
    gain_hbm,
    keys_hbm,
    values_hbm,
    w_out_hbm,
    router_hbm,
    shared_up_hbm,
    shared_down_hbm,
    up_hbm,
    down_hbm,
    out_ref,
    lengths_ref,
    routes_ref,
    query,
    key_new,
    value_new,
    hidden,
    gain,
    keys,
    values,
    w_out,
    router,
    shared_up,
    shared_down,
    ring,
    attended_all,
    hidden_all,
    unfold,
    projected_all,
    inner,
    normed_ref,
    gate_ref,
    shared_ref,
    own_ref,
    terms_buf,
    send_buf,
    recv_buf,
    local_sem,
    ring_sem,
    send_sem,
    recv_sem,
):
    me = lax.axis_index("expert")
    width = query.shape[1]
    units = up_hbm.shape[1]
    up_chunks = units // CHUNK
    piece = min(units, width)
    pieces = units // piece
    blocks = width // BLOCK
    total = up_chunks + blocks * pieces

    barrier = pltpu.get_barrier_semaphore()

    local = [
        pltpu.make_async_copy(src, dst, local_sem.at[i])
        for i, (src, dst) in enumerate(
            [
                (query_hbm, query),
                (key_new_hbm, key_new),
                (keys_hbm, keys),
                (values_hbm, values),
                (value_new_hbm, value_new),
                (hidden_hbm, hidden),
                (w_out_hbm, w_out),
                (gain_hbm, gain),
                (router_hbm, router),
                (shared_up_hbm, shared_up),
                (shared_down_hbm, shared_down),
                (lengths_hbm, lengths_ref),
                (routes_hbm, routes_ref),
            ]
        )
    ]
    (
        query_copy,
        key_new_copy,
        keys_copy,
        values_copy,
        value_new_copy,
        hidden_copy,
        w_out_copy,
        gain_copy,
        router_copy,
        shared_up_copy,
        shared_down_copy,
        lengths_copy,
        routes_copy,
    ) = local

    def up_copy(chunk, slot):
        return pltpu.make_async_copy(
            up_hbm.at[:, pl.ds(pl.multiple_of(chunk * CHUNK, CHUNK), CHUNK)],
            ring.at[slot],
            ring_sem.at[slot],
        )

    def down_copy(chunk, slot):
        block = chunk // pieces
        part = chunk - block * pieces
        return pltpu.make_async_copy(
            down_hbm.at[
                pl.ds(pl.multiple_of(part * piece, piece), piece),
                pl.ds(pl.multiple_of(block * BLOCK, BLOCK), BLOCK),
            ],
            ring.at[slot, pl.ds(0, piece), :],
            ring_sem.at[slot],
        )

    def chunk_copy(chunk):
        if chunk < up_chunks:
            return up_copy(chunk, chunk)
        return down_copy(chunk - up_chunks, chunk)

    issued = 0

    def start_chunks(last):
        nonlocal issued
        while issued < min(last, slots):
            chunk_copy(issued).start(priority=PRIORITY)
            issued += 1

    for copy in (query_copy, key_new_copy, keys_copy, values_copy, value_new_copy, hidden_copy, lengths_copy, routes_copy, w_out_copy):
        copy.start()
    start_chunks(EARLY)

    def greet(off, carry):
        pl.semaphore_signal(
            barrier, inc=1, device_id={"expert": lax.rem(me + off, n)}, device_id_type=MESH
        )
        return carry

    lax.fori_loop(1, n, greet, 0)

    rows = lax.broadcasted_iota(jnp.int32, (HEADS, width), 0)
    lanes = lax.broadcasted_iota(jnp.int32, (HEADS, width), 1)
    own_lane = lanes // HEAD_DIM == rows

    def fold(x):
        row = lax.broadcasted_iota(jnp.int32, (HEADS, HEAD_DIM), 0)
        taken = jnp.zeros((HEADS, HEAD_DIM), F32)
        for h in range(HEADS):
            taken = taken + jnp.where(row == h, x[:, h * HEAD_DIM : (h + 1) * HEAD_DIM], 0.0)
        return taken

    scale = 1.0 / math.sqrt(HEAD_DIM)
    query_copy.wait()
    key_new_copy.wait()
    spread_query = jnp.where(
        own_lane, jnp.broadcast_to(query[...].astype(F32), (HEADS, width)), 0.0
    )
    own_score = (
        jnp.sum(spread_query * key_new[...].astype(F32), axis=1, keepdims=True) * scale
    )
    spread_query = spread_query.astype(BF16)
    keys_copy.wait()
    scores = (
        lax.dot_general(
            spread_query, keys[...], (((1,), (1,)), ((), ())), preferred_element_type=F32
        )
        * scale
    )
    lengths_copy.wait()
    values_copy.wait()
    value_new_copy.wait()
    hidden_copy.wait()
    for copy in (gain_copy, router_copy, shared_up_copy, shared_down_copy):
        copy.start()
    start_chunks(slots)

    position = lax.broadcasted_iota(jnp.int32, scores.shape, 1)
    scores = jnp.where(position < lengths_ref[0], scores, -1e30)
    top = jnp.maximum(jnp.max(scores, axis=1, keepdims=True), own_score)
    weights = jnp.exp(scores - top)
    own_weight = jnp.exp(own_score - top)
    normalizer = jnp.sum(weights, axis=1, keepdims=True) + own_weight
    weights = (weights / normalizer).astype(BF16)
    own_weight = (own_weight / normalizer).astype(BF16).astype(F32)
    mixed = jnp.dot(weights, values[...], preferred_element_type=F32)
    mixed = mixed + own_weight * value_new[...].astype(F32)
    mine = pl.ds(pl.multiple_of(me * HEADS, HEADS), HEADS)
    attended_all[mine, :] = fold(mixed).astype(BF16)
    hidden_all[mine, :] = fold(
        jnp.broadcast_to(hidden[...].astype(F32), (HEADS, width))
    ).astype(BF16)

    pl.semaphore_wait(barrier, n - 1)

    def send_all(src, dst, sem):
        def send(off, carry):
            pltpu.make_async_remote_copy(
                src_ref=src,
                dst_ref=dst,
                send_sem=send_sem.at[sem],
                recv_sem=recv_sem.at[sem],
                device_id={"expert": lax.rem(me + off, n)},
                device_id_type=MESH,
            ).start()
            return carry

        lax.fori_loop(1, n, send, 0)

    def await_bytes(ref, sem):
        pltpu.make_async_copy(ref, ref, sem).wait()

    send_all(attended_all.at[mine, :], attended_all.at[mine, :], 0)
    send_all(hidden_all.at[mine, :], hidden_all.at[mine, :], 1)

    others = pl.ds(0, (n - 1) * HEADS)
    await_bytes(attended_all.at[others, :], recv_sem.at[0])
    unfold[...] = attended_all[...].astype(F32)
    attended = jnp.concatenate(
        [unfold[pl.ds(h, n, stride=HEADS), :].astype(BF16) for h in range(HEADS)], axis=1
    )
    w_out_copy.wait()
    projected = jnp.dot(attended, w_out[...], preferred_element_type=F32).astype(BF16)
    cols = projected.shape[1]
    my_cols = pl.ds(pl.multiple_of(me * cols, cols), cols)
    if cols % 128 == 0:
        projected_all[:, my_cols] = projected
        piece_ref = projected_all.at[:, my_cols]
        arrived = projected_all.at[:, pl.ds(0, (n - 1) * cols)]
    else:
        projected_all[me] = projected
        piece_ref = projected_all.at[me]
        arrived = projected_all.at[pl.ds(0, n - 1)]
    send_all(piece_ref, piece_ref, 2)
    await_bytes(hidden_all.at[others, :], recv_sem.at[1])
    unfold[...] = hidden_all[...].astype(F32)
    every_hidden = jnp.concatenate(
        [unfold[pl.ds(h, n, stride=HEADS), :] for h in range(HEADS)], axis=1
    )
    routes_copy.wait()
    token = lax.broadcasted_iota(jnp.int32, (n, 1), 0)
    chosen_expert = jnp.zeros((n, 1), jnp.int32)
    for t in range(n):
        chosen_expert = jnp.where(token == t, routes_ref[t], chosen_expert)
    gain_copy.wait()
    router_copy.wait()
    await_bytes(arrived, recv_sem.at[2])
    if cols % 128 == 0:
        every_projected = projected_all[...].astype(F32)
    else:
        every_projected = jnp.concatenate(
            [projected_all[d].astype(F32) for d in range(n)], axis=1
        )
    residual = every_hidden + every_projected
    centered = residual - jnp.mean(residual, axis=1, keepdims=True)
    variance = jnp.mean(centered * centered, axis=1, keepdims=True)
    normed = (
        centered / jnp.sqrt(jnp.maximum(variance, 0.25)) * gain[...].astype(F32).reshape(1, width)
    ).astype(BF16)
    normed_ref[...] = normed
    own_ref[...] = jnp.sum(jnp.where(token == me, residual, 0.0), axis=0, keepdims=True)

    shared_up_copy.wait()
    shared_ref[...] = gelu(
        jnp.dot(normed_ref[...], shared_up[...], preferred_element_type=F32)
    ).astype(BF16)
    logits = lax.dot_general(
        normed_ref[...], router[...], (((1,), (1,)), ((), ())), preferred_element_type=F32
    )
    expert_ids = lax.broadcasted_iota(jnp.int32, logits.shape, 1)
    chosen = jnp.sum(jnp.where(chosen_expert == expert_ids, logits, 0.0), axis=1, keepdims=True)
    gate_ref[...] = 1.0 / (1.0 + jnp.exp(-chosen))

    together = math.gcd(TOGETHER, up_chunks)

    def up_step(step, carry):
        chunks = [step * together + i for i in range(together)]
        for chunk in chunks:
            up_copy(chunk, chunk).wait()
        for chunk in chunks:
            act = gelu(jnp.dot(normed_ref[...], ring[chunk], preferred_element_type=F32))
            expert = (me * units + chunk * CHUNK) // FF
            inner[:, pl.ds(pl.multiple_of(chunk * CHUNK, CHUNK), CHUNK)] = jnp.where(
                chosen_expert == expert, act, 0.0
            ).astype(BF16)
        for chunk in chunks:

            @pl.when(chunk + slots < total)
            def _(chunk=chunk):
                down_copy(chunk + slots - up_chunks, chunk).start(priority=PRIORITY)

        return carry

    lax.fori_loop(0, up_chunks // together, up_step, 0)
    shared_down_copy.wait()

    group_rows = GROUP_COLS // 128
    groups = width // GROUP_COLS
    blocks_per_group = blocks // groups

    for group in range(groups):

        def down_step(index, carry, group=group):
            block = group * blocks_per_group + index
            acc = jnp.zeros((n, BLOCK), F32)
            first = up_chunks + block * pieces
            held = [lax.rem(first + part, slots) for part in range(pieces)]
            for part in range(pieces):
                if part % JOINT == 0:
                    for later in range(part, min(part + JOINT, pieces)):
                        down_copy(first + later - up_chunks, held[later]).wait()
                acc = acc + jnp.dot(
                    inner[:, pl.ds(part * piece, piece)],
                    ring[held[part], pl.ds(0, piece), :],
                    preferred_element_type=F32,
                )
            shared = jnp.dot(
                shared_ref[...],
                shared_down[:, pl.ds(pl.multiple_of(block * BLOCK, BLOCK), BLOCK)],
                preferred_element_type=F32,
            )
            terms = shared + gate_ref[...] * acc
            for k in range(BLOCK // 128):
                row = index * (BLOCK // 128) + k
                terms_buf[pl.ds(row, n, stride=group_rows), :] = terms[:, k * 128 : (k + 1) * 128]
            return carry

        lax.fori_loop(0, blocks_per_group, down_step, 0)
        send_buf[group] = terms_buf[...].reshape(n, group_rows, 128).astype(BF16)

        def send_terms(off, carry, group=group):
            peer = lax.rem(me + off, n)
            pltpu.make_async_remote_copy(
                src_ref=send_buf.at[group, peer],
                dst_ref=recv_buf.at[group, me],
                send_sem=send_sem.at[3 + group],
                recv_sem=recv_sem.at[3 + group],
                device_id={"expert": peer},
                device_id_type=MESH,
            ).start()
            return carry

        lax.fori_loop(1, n, send_terms, 0)
        recv_buf[group, me] = send_buf[group, me]

    for group in range(groups):
        landed = recv_buf.at[group, pl.ds(0, n - 1)]
        await_bytes(landed, recv_sem.at[3 + group])
        summed = jnp.zeros((group_rows, 128), F32)
        for d in range(n):
            summed = summed + recv_buf[group, d].astype(F32)
        for j in range(group_rows):
            where = pl.ds(group * GROUP_COLS + j * 128, 128)
            out_ref[:, where] = (own_ref[:, where] + summed[j : j + 1, :]).astype(out_ref.dtype)

    await_bytes(attended_all.at[others, :], send_sem.at[0])
    await_bytes(hidden_all.at[others, :], send_sem.at[1])
    await_bytes(arrived, send_sem.at[2])
    for group in range(groups):
        sent = send_buf.at[group, pl.ds(0, n - 1)]
        await_bytes(sent, send_sem.at[3 + group])


def solution(mesh):
    n = mesh.shape["expert"]

    def body(
        query,
        key_new,
        value_new,
        key_cache,
        value_cache,
        lengths,
        hidden,
        routes,
        w_out,
        ln_gain,
        router,
        shared_up,
        shared_down,
        expert_up,
        expert_down,
    ):
        assert query.shape[0] == 1
        width = query.shape[1]
        units = expert_up.shape[1]
        cache = key_cache.shape[1]
        shared_units = shared_up.shape[1]
        cols = w_out.shape[1]
        piece = min(units, width)
        total = units // CHUNK + (width // BLOCK) * (units // piece)
        slots = min(MAX_SLOTS, total)
        groups = width // GROUP_COLS
        rows_sent = GROUP_COLS // 128
        gathered = (n, width) if cols % 128 == 0 else (n, n, cols)
        vmem = pltpu.VMEM
        hbm = pl.BlockSpec(memory_space=pl.ANY)
        return pl.pallas_call(
            functools.partial(kernel, n, slots),
            out_shape=pltpu.VMEM((1, width), BF16),
            in_specs=[hbm] * 15,
            out_specs=pl.BlockSpec(memory_space=pltpu.VMEM),
            scratch_shapes=[
                pltpu.SMEM(lengths.shape, jnp.int32),
                pltpu.SMEM(routes.shape, jnp.int32),
                vmem((1, width), BF16),
                vmem((1, width), BF16),
                vmem((1, width), BF16),
                vmem((1, width), BF16),
                vmem((width,), BF16),
                vmem((cache, width), BF16),
                vmem((cache, width), BF16),
                vmem((width, cols), BF16),
                vmem((EXPERTS, width), BF16),
                vmem((width, shared_units), BF16),
                vmem((shared_units, width), BF16),
                vmem((slots, width, CHUNK), BF16),
                vmem((n * HEADS, HEAD_DIM), BF16),
                vmem((n * HEADS, HEAD_DIM), BF16),
                vmem((n * HEADS, HEAD_DIM), F32),
                vmem(gathered, BF16),
                vmem((n, units), BF16),
                vmem((n, width), BF16),
                vmem((n, 1), F32),
                vmem((n, shared_units), BF16),
                vmem((1, width), F32),
                vmem((n * rows_sent, 128), F32),
                vmem((groups, n, rows_sent, 128), BF16),
                vmem((groups, n, rows_sent, 128), BF16),
                pltpu.SemaphoreType.DMA((13,)),
                pltpu.SemaphoreType.DMA((slots,)),
                pltpu.SemaphoreType.DMA((3 + groups,)),
                pltpu.SemaphoreType.DMA((3 + groups,)),
            ],
            compiler_params=pltpu.CompilerParams(
                collective_id=0, has_side_effects=True, vmem_limit_bytes=66_900_000
            ),
        )(
            lengths,
            routes,
            query,
            key_new,
            value_new,
            hidden,
            ln_gain,
            key_cache.reshape(cache, width),
            value_cache.reshape(cache, width),
            w_out,
            router.T,
            shared_up,
            shared_down,
            expert_up,
            expert_down,
        )

    rows = P(("group", "expert"), None)
    placed = (
        rows,
        rows,
        rows,
        P(("group", "expert"), None, None),
        P(("group", "expert"), None, None),
        P(("group", "expert")),
        rows,
        P("group"),
        P(None, "expert"),
        P(),
        P(),
        P(None, "expert"),
        P("expert", None),
        P(None, "expert"),
        P("expert", None),
    )
    return jax.shard_map(body, mesh=mesh, in_specs=placed, out_specs=rows, check_vma=False)
```

profile of v0, /device:TPU:0, one launch (start us, length us, event | category | flops | bytes accessed | tf_op | source)
XLA Modules:
  0.0 32.9 jit_solution(188807805122993554)
XLA Ops:
  0.7 31.7 %shard_map.145 = bf16[1,2048]{1,0:T(2,128)(2,1)S(1)} custom-call(s32[1]{0:T(128)S(6)} %copy.18.lengths_hbm, s32[16]{0:T(128)} %routes_hbm.1, bf16[1,2048]{1,0:T(2,128)(2,1)} %query_hbm.1, bf16[1,2048]{1,0:T(2,128)(2,1)} %key_new_hbm.1, bf16[1,2048]{1,0:T(2,128)(2,1)} %value_new_hbm.1, bf16[1,2048]{1,0:T(2,128)(2,1)} %hidden_hbm.1, bf16[2048]{0:T(1024)(128)(2,1)} %gain_hbm.1, ...), custom_call_target="tpu_custom_call" | custom-call | tf_op jit(solution)/shard_map/pallas_call | solution.py:429
  32.3 0.6 %copy.17 = bf16[1,2048]{1,0:T(2,128)(2,1)} copy(bf16[1,2048]{1,0:T(2,128)(2,1)S(1)} %shard_map.145) | data formatting | bytes 8192
where the time goes:
time: 33.1 us; the launch traced here: 32.9 us
  Pallas kernels  31.7 us (96%)
  between operations  0.66 us (2%)
  local copies, waits for them, and re-layouts  0.6 us (2%)
    pallas_call x1, Pallas kernels, body(): pl.pallas_call(functools.partial(kernel, n, slots), out_shape=pltpu.VMEM(...  31.7 us

commit v1 on v0

v1 whole, which is shorter than its diff:
```python
import functools
import math

import jax
import jax.numpy as jnp
from jax import lax
from jax.experimental import pallas as pl
from jax.experimental.pallas import tpu as pltpu
from jax.sharding import PartitionSpec as P

HEADS = 16
HEAD_DIM = 128
FF = 4096
EXPERTS = 32
CHUNK = 512
BLOCK = 512
EARLY = 3
PRIORITY = 1
TOGETHER = 4
GROUP_COLS = 1024
MESH = pl.DeviceIdType.MESH
F32 = jnp.float32
BF16 = jnp.bfloat16


def gelu(v):
    return 0.5 * v * (1.0 + jnp.tanh(math.sqrt(2.0 / math.pi) * (v + 0.044715 * (v * v * v))))


def kernel(
    replicas,
    n,
    lengths_hbm,
    routes_hbm,
    query_hbm,
    key_new_hbm,
    value_new_hbm,
    hidden_hbm,
    gain_hbm,
    keys_hbm,
    values_hbm,
    w_out_hbm,
    router_hbm,
    shared_up_hbm,
    shared_down_hbm,
    up_hbm,
    down_hbm,
    out_ref,
    lengths_ref,
    routes_all,
    query,
    key_new,
    value_new,
    hidden,
    gain,
    keys,
    values,
    w_out,
    router,
    shared_up,
    shared_down,
    up,
    down,
    attended_all,
    hidden_all,
    unfold,
    projected_all,
    inner,
    normed_ref,
    gate_ref,
    shared_ref,
    own_ref,
    terms_buf,
    send_buf,
    recv_buf,
    local_sem,
    up_sem,
    down_sem,
    send_sem,
    recv_sem,
):
    mine_g = lax.axis_index("group")
    me = lax.axis_index("expert")
    world = replicas * n
    rank = mine_g * n + me
    width = query.shape[1]
    units = up_hbm.shape[1]
    share = units // replicas
    chunk_cols = up.shape[2]
    up_chunks = up.shape[0]
    block_cols = down.shape[2]
    blocks = down.shape[0]
    piece = min(share, width)
    pieces = share // piece
    shared_units = shared_up_hbm.shape[1]
    shared_share = shared_up.shape[1]

    barrier = pltpu.get_barrier_semaphore()

    if shared_share == shared_units:
        shared_up_src, shared_down_src = shared_up_hbm, shared_down_hbm
    else:
        my_shared = pl.ds(pl.multiple_of(mine_g * shared_share, shared_share), shared_share)
        shared_up_src = shared_up_hbm.at[:, my_shared]
        shared_down_src = shared_down_hbm.at[my_shared, :]

    local = [
        pltpu.make_async_copy(src, dst, local_sem.at[i])
        for i, (src, dst) in enumerate(
            [
                (query_hbm, query),
                (key_new_hbm, key_new),
                (keys_hbm, keys),
                (values_hbm, values),
                (value_new_hbm, value_new),
                (hidden_hbm, hidden),
                (w_out_hbm, w_out),
                (gain_hbm, gain),
                (router_hbm, router),
                (shared_up_src, shared_up),
                (shared_down_src, shared_down),
                (lengths_hbm, lengths_ref),
                (routes_hbm, routes_all.at[mine_g]),
            ]
        )
    ]
    (
        query_copy,
        key_new_copy,
        keys_copy,
        values_copy,
        value_new_copy,
        hidden_copy,
        w_out_copy,
        gain_copy,
        router_copy,
        shared_up_copy,
        shared_down_copy,
        lengths_copy,
        routes_copy,
    ) = local

    def up_copy(chunk):
        first = mine_g * share + chunk * chunk_cols
        return pltpu.make_async_copy(
            up_hbm.at[:, pl.ds(pl.multiple_of(first, chunk_cols), chunk_cols)],
            up.at[chunk],
            up_sem.at[chunk],
        )

    def down_copy(block, part):
        first = mine_g * share + part * piece
        return pltpu.make_async_copy(
            down_hbm.at[
                pl.ds(pl.multiple_of(first, piece), piece),
                pl.ds(block * block_cols, block_cols),
            ],
            down.at[block, pl.ds(part * piece, piece), :],
            down_sem.at[block * pieces + part],
        )

    chunk_copies = [up_copy(c) for c in range(up_chunks)] + [
        down_copy(b, p) for b in range(blocks) for p in range(pieces)
    ]
    issued = 0

    def start_chunks(last):
        nonlocal issued
        while issued < min(last, len(chunk_copies)):
            chunk_copies[issued].start(priority=PRIORITY)
            issued += 1

    for copy in (query_copy, key_new_copy, keys_copy, values_copy, value_new_copy, hidden_copy, lengths_copy, routes_copy, w_out_copy):
        copy.start()
    start_chunks(EARLY)

    def place(peer):
        return {"group": peer // n, "expert": lax.rem(peer, n)}

    def greet(off, carry):
        pl.semaphore_signal(
            barrier, inc=1, device_id=place(lax.rem(rank + off, world)), device_id_type=MESH
        )
        return carry

    lax.fori_loop(1, world, greet, 0)

    rows = lax.broadcasted_iota(jnp.int32, (HEADS, width), 0)
    lanes = lax.broadcasted_iota(jnp.int32, (HEADS, width), 1)
    own_lane = lanes // HEAD_DIM == rows

    def fold(x):
        row = lax.broadcasted_iota(jnp.int32, (HEADS, HEAD_DIM), 0)
        taken = jnp.zeros((HEADS, HEAD_DIM), F32)
        for h in range(HEADS):
            taken = taken + jnp.where(row == h, x[:, h * HEAD_DIM : (h + 1) * HEAD_DIM], 0.0)
        return taken

    scale = 1.0 / math.sqrt(HEAD_DIM)
    query_copy.wait()
    key_new_copy.wait()
    spread_query = jnp.where(
        own_lane, jnp.broadcast_to(query[...].astype(F32), (HEADS, width)), 0.0
    )
    own_score = (
        jnp.sum(spread_query * key_new[...].astype(F32), axis=1, keepdims=True) * scale
    )
    spread_query = spread_query.astype(BF16)
    mine = pl.ds(pl.multiple_of(me * HEADS, HEADS), HEADS)
    hidden_copy.wait()
    hidden_all[mine_g, mine, :] = fold(
        jnp.broadcast_to(hidden[...].astype(F32), (HEADS, width))
    ).astype(BF16)
    keys_copy.wait()
    scores = (
        lax.dot_general(
            spread_query, keys[...], (((1,), (1,)), ((), ())), preferred_element_type=F32
        )
        * scale
    )
    lengths_copy.wait()
    values_copy.wait()
    value_new_copy.wait()
    for copy in (gain_copy, router_copy, shared_up_copy, shared_down_copy):
        copy.start()
    start_chunks(len(chunk_copies))

    position = lax.broadcasted_iota(jnp.int32, scores.shape, 1)
    scores = jnp.where(position < lengths_ref[0], scores, -1e30)
    top = jnp.maximum(jnp.max(scores, axis=1, keepdims=True), own_score)
    weights = jnp.exp(scores - top)
    own_weight = jnp.exp(own_score - top)
    normalizer = jnp.sum(weights, axis=1, keepdims=True) + own_weight
    weights = (weights / normalizer).astype(BF16)
    own_weight = (own_weight / normalizer).astype(BF16).astype(F32)
    mixed = jnp.dot(weights, values[...], preferred_element_type=F32)
    mixed = mixed + own_weight * value_new[...].astype(F32)
    attended_all[mine, :] = fold(mixed).astype(BF16)
    routes_copy.wait()

    pl.semaphore_wait(barrier, world - 1)

    def send(src, dst, sem, to):
        pltpu.make_async_remote_copy(
            src_ref=src,
            dst_ref=dst,
            send_sem=send_sem.at[sem],
            recv_sem=recv_sem.at[sem],
            device_id=to,
            device_id_type=MESH,
        ).start()

    def send_group(ref, sem):
        def step(off, carry):
            send(ref, ref, sem, {"expert": lax.rem(me + off, n)})
            return carry

        lax.fori_loop(1, n, step, 0)

    def send_twins(ref, sem):
        for off in range(1, replicas):
            send(ref, ref, sem, {"group": lax.rem(mine_g + off, replicas)})

    def send_others(ref, sem):
        for other in range(1, replicas):

            def step(off, carry, other=other):
                group = lax.rem(mine_g + other, replicas)
                send(ref, ref, sem, {"group": group, "expert": lax.rem(me + off, n)})
                return carry

            lax.fori_loop(0, n, step, 0)

    def await_bytes(ref, sem):
        pltpu.make_async_copy(ref, ref, sem).wait()

    attended_piece = attended_all.at[mine, :]
    send_group(attended_piece, 0)
    send_group(hidden_all.at[mine_g, mine, :], 1)
    send_twins(routes_all.at[mine_g], 2)

    others = pl.ds(0, (n - 1) * HEADS)
    token = lax.broadcasted_iota(jnp.int32, (world, 1), 0)
    await_bytes(hidden_all.at[0, others, :], recv_sem.at[1])
    send_twins(hidden_all.at[mine_g], 3)
    await_bytes(attended_all.at[others, :], recv_sem.at[0])
    unfold[pl.ds(0, n * HEADS), :] = attended_all[...].astype(F32)
    attended = jnp.concatenate(
        [unfold[pl.ds(h, n, stride=HEADS), :].astype(BF16) for h in range(HEADS)], axis=1
    )
    w_out_copy.wait()
    projected = jnp.dot(attended, w_out[...], preferred_element_type=F32).astype(BF16)
    cols = projected.shape[1]
    my_cols = pl.ds(pl.multiple_of(me * cols, cols), cols)
    if cols % 128 == 0:
        projected_all[mine_g, :, my_cols] = projected
        piece_ref = projected_all.at[mine_g, :, my_cols]
        near = projected_all.at[0, :, pl.ds(0, (n - 1) * cols)]
    else:
        projected_all[mine_g, me] = projected
        piece_ref = projected_all.at[mine_g, me]
        near = projected_all.at[0, pl.ds(0, n - 1)]
    far = projected_all.at[pl.ds(0, replicas - 1)]
    send_group(piece_ref, 4)
    send_others(piece_ref, 5)

    twins = pl.ds(0, replicas - 1)
    await_bytes(routes_all.at[twins], recv_sem.at[2])
    square = (n, n)
    on_diagonal = lax.broadcasted_iota(jnp.int32, square, 0) == lax.broadcasted_iota(
        jnp.int32, square, 1
    )
    chosen_expert = jnp.concatenate(
        [
            jnp.sum(
                jnp.where(on_diagonal, jnp.broadcast_to(routes_all[i].astype(F32), square), 0.0),
                axis=1,
                keepdims=True,
            )
            for i in range(replicas)
        ],
        axis=0,
    )
    gain_copy.wait()
    router_copy.wait()
    expert_ids = lax.broadcasted_iota(jnp.int32, (world, EXPERTS), 1).astype(F32)
    chosen_router = jnp.dot(
        jnp.where(chosen_expert == expert_ids, 1.0, 0.0).astype(BF16),
        router[...],
        preferred_element_type=F32,
    )
    await_bytes(hidden_all.at[twins], recv_sem.at[3])
    unfold[...] = hidden_all[...].reshape(world * HEADS, HEAD_DIM).astype(F32)
    every_hidden = jnp.concatenate(
        [unfold[pl.ds(h, world, stride=HEADS), :] for h in range(HEADS)], axis=1
    )
    await_bytes(near, recv_sem.at[4])
    await_bytes(far, recv_sem.at[5])
    if cols % 128 == 0:
        every_projected = projected_all[...].reshape(world, width).astype(F32)
    else:
        every_projected = jnp.concatenate(
            [
                jnp.concatenate([projected_all[i, d].astype(F32) for d in range(n)], axis=1)
                for i in range(replicas)
            ],
            axis=0,
        )
    residual = every_hidden + every_projected
    centered = residual - jnp.mean(residual, axis=1, keepdims=True)
    variance = jnp.mean(centered * centered, axis=1, keepdims=True)
    normed = (
        centered / jnp.sqrt(jnp.maximum(variance, 0.25)) * gain[...].astype(F32).reshape(1, width)
    ).astype(BF16)
    normed_ref[...] = normed
    own_ref[...] = jnp.sum(jnp.where(token == rank, residual, 0.0), axis=0, keepdims=True)
    chosen = jnp.sum(normed.astype(F32) * chosen_router, axis=1, keepdims=True)
    gate_ref[...] = 1.0 / (1.0 + jnp.exp(-chosen))

    shared_up_copy.wait()
    shared_act = gelu(jnp.dot(normed_ref[...], shared_up[...], preferred_element_type=F32))
    if shared_share == shared_units:
        unit = lax.broadcasted_iota(jnp.int32, shared_act.shape, 1)
        shared_act = jnp.where(unit // (shared_units // replicas) == mine_g, shared_act, 0.0)
    shared_ref[...] = shared_act.astype(BF16)

    together = math.gcd(TOGETHER, up_chunks)

    def up_step(step, carry):
        chunks = [step * together + i for i in range(together)]
        for chunk in chunks:
            up_copy(chunk).wait()
        for chunk in chunks:
            act = gelu(jnp.dot(normed_ref[...], up[chunk], preferred_element_type=F32))
            expert = (me * units + mine_g * share + chunk * chunk_cols) // FF
            inner[:, pl.ds(pl.multiple_of(chunk * chunk_cols, chunk_cols), chunk_cols)] = jnp.where(
                chosen_expert == expert.astype(F32), act, 0.0
            ).astype(BF16)
        return carry

    lax.fori_loop(0, up_chunks // together, up_step, 0)
    shared_down_copy.wait()

    group_rows = GROUP_COLS // 128
    groups = width // GROUP_COLS
    blocks_per_group = blocks // groups

    for group in range(groups):
        for index in range(blocks_per_group):
            block = group * blocks_per_group + index
            for part in range(pieces):
                down_copy(block, part).wait()
            acc = jnp.dot(inner[...], down[block], preferred_element_type=F32)
            shared = jnp.dot(
                shared_ref[...],
                shared_down[:, pl.ds(block * block_cols, block_cols)],
                preferred_element_type=F32,
            )
            terms = shared + gate_ref[...] * acc
            for k in range(block_cols // 128):
                row = index * (block_cols // 128) + k
                terms_buf[pl.ds(row, world, stride=group_rows), :] = terms[:, k * 128 : (k + 1) * 128]
        send_buf[group] = terms_buf[...].reshape(world, group_rows, 128).astype(BF16)

        def send_terms(off, carry, group=group):
            peer = lax.rem(rank + off, world)
            send(send_buf.at[group, peer], recv_buf.at[group, rank], 6 + group, place(peer))
            return carry

        lax.fori_loop(1, world, send_terms, 0)
        recv_buf[group, rank] = send_buf[group, rank]

    for group in range(groups):
        landed = recv_buf.at[group, pl.ds(0, world - 1)]
        await_bytes(landed, recv_sem.at[6 + group])
        summed = jnp.zeros((group_rows, 128), F32)
        for d in range(world):
            summed = summed + recv_buf[group, d].astype(F32)
        for j in range(group_rows):
            where = pl.ds(group * GROUP_COLS + j * 128, 128)
            out_ref[:, where] = (own_ref[:, where] + summed[j : j + 1, :]).astype(out_ref.dtype)

    await_bytes(attended_all.at[others, :], send_sem.at[0])
    await_bytes(hidden_all.at[0, others, :], send_sem.at[1])
    await_bytes(routes_all.at[twins], send_sem.at[2])
    await_bytes(hidden_all.at[twins], send_sem.at[3])
    await_bytes(near, send_sem.at[4])
    await_bytes(far, send_sem.at[5])
    for group in range(groups):
        sent = send_buf.at[group, pl.ds(0, world - 1)]
        await_bytes(sent, send_sem.at[6 + group])


def solution(mesh):
    n = mesh.shape["expert"]
    replicas = mesh.shape["group"]
    world = n * replicas

    def body(
        query,
        key_new,
        value_new,
        key_cache,
        value_cache,
        lengths,
        hidden,
        routes,
        w_out,
        ln_gain,
        router,
        shared_up,
        shared_down,
        expert_up,
        expert_down,
    ):
        assert query.shape[0] == 1
        width = query.shape[1]
        share = expert_up.shape[1] // replicas
        cache = key_cache.shape[1]
        shared_share = shared_up.shape[1] // replicas
        if shared_share % 128:
            shared_share = shared_up.shape[1]
        cols = w_out.shape[1]
        chunk_cols = min(CHUNK, share)
        up_chunks = share // chunk_cols
        blocks = width // BLOCK
        pieces = share // min(share, width)
        groups = width // GROUP_COLS
        rows_sent = GROUP_COLS // 128
        gathered = (replicas, n, width) if cols % 128 == 0 else (replicas, n, n, cols)
        vmem = pltpu.VMEM
        hbm = pl.BlockSpec(memory_space=pl.ANY)
        return pl.pallas_call(
            functools.partial(kernel, replicas, n),
            out_shape=pltpu.VMEM((1, width), BF16),
            in_specs=[hbm] * 15,
            out_specs=pl.BlockSpec(memory_space=pltpu.VMEM),
            scratch_shapes=[
                pltpu.SMEM(lengths.shape, jnp.int32),
                vmem((replicas, 1, n), jnp.int32),
                vmem((1, width), BF16),
                vmem((1, width), BF16),
                vmem((1, width), BF16),
                vmem((1, width), BF16),
                vmem((width,), BF16),
                vmem((cache, width), BF16),
                vmem((cache, width), BF16),
                vmem((width, cols), BF16),
                vmem((EXPERTS, width), BF16),
                vmem((width, shared_share), BF16),
                vmem((shared_share, width), BF16),
                vmem((up_chunks, width, chunk_cols), BF16),
                vmem((blocks, share, BLOCK), BF16),
                vmem((n * HEADS, HEAD_DIM), BF16),
                vmem((replicas, n * HEADS, HEAD_DIM), BF16),
                vmem((world * HEADS, HEAD_DIM), F32),
                vmem(gathered, BF16),
                vmem((world, share), BF16),
                vmem((world, width), BF16),
                vmem((world, 1), F32),
                vmem((world, shared_share), BF16),
                vmem((1, width), F32),
                vmem((world * rows_sent, 128), F32),
                vmem((groups, world, rows_sent, 128), BF16),
                vmem((groups, world, rows_sent, 128), BF16),
                pltpu.SemaphoreType.DMA((13,)),
                pltpu.SemaphoreType.DMA((up_chunks,)),
                pltpu.SemaphoreType.DMA((blocks * pieces,)),
                pltpu.SemaphoreType.DMA((6 + groups,)),
                pltpu.SemaphoreType.DMA((6 + groups,)),
            ],
            compiler_params=pltpu.CompilerParams(
                collective_id=0, has_side_effects=True, vmem_limit_bytes=66_900_000
            ),
        )(
            lengths,
            routes.reshape(1, n),
            query,
            key_new,
            value_new,
            hidden,
            ln_gain,
            key_cache.reshape(cache, width),
            value_cache.reshape(cache, width),
            w_out,
            router.T,
            shared_up,
            shared_down,
            expert_up,
            expert_down,
        )

    rows = P(("group", "expert"), None)
    placed = (
        rows,
        rows,
        rows,
        P(("group", "expert"), None, None),
        P(("group", "expert"), None, None),
        P(("group", "expert")),
        rows,
        P("group"),
        P(None, "expert"),
        P(),
        P(),
        P(None, "expert"),
        P("expert", None),
        P(None, "expert"),
        P("expert", None),
    )
    return jax.shard_map(body, mesh=mesh, in_specs=placed, out_specs=rows, check_vma=False)
```

time: 33.1 us -> 31.9 us (0.964)
  Pallas kernels: 31.7 us -> 30.4 us
    pallas_call x1, Pallas kernels: 31.7 us -> 30.4 us  [body(): pl.pallas_call(functools.partial(kernel, replicas, n), out_shape=pltpu.VM...]
where the time goes in v1:
time: 31.9 us; the launch traced here: 31.7 us
  Pallas kernels  30.4 us (95%)
  between operations  0.66 us (2%)
  local copies, waits for them, and re-layouts  0.6 us (2%)
    pallas_call x1, Pallas kernels, body(): pl.pallas_call(functools.partial(kernel, replicas, n), out_shape=pltpu.VM...  30.4 us

profile of v1, /device:TPU:0, one launch (start us, length us, event | category | flops | bytes accessed | tf_op | source)
XLA Modules:
  0.0 31.7 jit_solution(5080136720026769150)
XLA Ops:
  0.7 30.4 %shard_map.145 = bf16[1,2048]{1,0:T(2,128)(2,1)S(1)} custom-call(s32[1]{0:T(128)S(6)} %copy.18.lengths_hbm, s32[1,16]{1,0:T(1,128)} %bitcast.7, bf16[1,2048]{1,0:T(2,128)(2,1)} %query_hbm.1, bf16[1,2048]{1,0:T(2,128)(2,1)} %key_new_hbm.1, bf16[1,2048]{1,0:T(2,128)(2,1)} %value_new_hbm.1, bf16[1,2048]{1,0:T(2,128)(2,1)} %hidden_hbm.1, ...), custom_call_target="tpu_custom_call" | custom-call | tf_op jit(solution)/shard_map/pallas_call | solution.py:473
  31.1 0.6 %copy.17 = bf16[1,2048]{1,0:T(2,128)(2,1)} copy(bf16[1,2048]{1,0:T(2,128)(2,1)S(1)} %shard_map.145) | data formatting | bytes 8192

commit v2 on v1

--- a/solution.py
+++ b/solution.py
@@ -16,7 +16,8 @@
 BLOCK = 512
 EARLY = 3
 PRIORITY = 1
-TOGETHER = 4
+UNROLL = 32
+MOST_ROUTED = 8
 GROUP_COLS = 1024
 MESH = pl.DeviceIdType.MESH
 F32 = jnp.float32
@@ -65,6 +66,11 @@
     hidden_all,
     unfold,
     projected_all,
+    picked_hidden,
+    guest_hidden,
+    picked_projected,
+    guest_projected,
+    guests_ref,
     inner,
     normed_ref,
     gate_ref,
@@ -92,17 +98,14 @@
     blocks = down.shape[0]
     piece = min(share, width)
     pieces = share // piece
-    shared_units = shared_up_hbm.shape[1]
-    shared_share = shared_up.shape[1]
+    slots = guest_hidden.shape[1]
+    served = guests_ref.shape[0]
+    cols = w_out.shape[1]
+
+    def expert_of(group, device):
+        return (device * units + group * share) // FF
 
     barrier = pltpu.get_barrier_semaphore()
-
-    if shared_share == shared_units:
-        shared_up_src, shared_down_src = shared_up_hbm, shared_down_hbm
-    else:
-        my_shared = pl.ds(pl.multiple_of(mine_g * shared_share, shared_share), shared_share)
-        shared_up_src = shared_up_hbm.at[:, my_shared]
-        shared_down_src = shared_down_hbm.at[my_shared, :]
 
     local = [
         pltpu.make_async_copy(src, dst, local_sem.at[i])
@@ -117,8 +120,8 @@
                 (w_out_hbm, w_out),
                 (gain_hbm, gain),
                 (router_hbm, router),
-                (shared_up_src, shared_up),
-                (shared_down_src, shared_down),
+                (shared_up_hbm, shared_up),
+                (shared_down_hbm, shared_down),
                 (lengths_hbm, lengths_ref),
                 (routes_hbm, routes_all.at[mine_g]),
             ]
@@ -159,7 +162,7 @@
             down_sem.at[block * pieces + part],
         )
 
-    chunk_copies = [up_copy(c) for c in range(up_chunks)] + [
+    chunk_copies = [up_copy(c) for c in range(up_chunks)] + [shared_down_copy] + [
         down_copy(b, p) for b in range(blocks) for p in range(pieces)
     ]
     issued = 0
@@ -208,7 +211,7 @@
     spread_query = spread_query.astype(BF16)
     mine = pl.ds(pl.multiple_of(me * HEADS, HEADS), HEADS)
     hidden_copy.wait()
-    hidden_all[mine_g, mine, :] = fold(
+    hidden_all[mine, :] = fold(
         jnp.broadcast_to(hidden[...].astype(F32), (HEADS, width))
     ).astype(BF16)
     keys_copy.wait()
@@ -221,7 +224,7 @@
     lengths_copy.wait()
     values_copy.wait()
     value_new_copy.wait()
-    for copy in (gain_copy, router_copy, shared_up_copy, shared_down_copy):
+    for copy in (gain_copy, router_copy, shared_up_copy):
         copy.start()
     start_chunks(len(chunk_copies))
 
@@ -250,165 +253,238 @@
             device_id_type=MESH,
         ).start()
 
+    def loop(count, step):
+        if count <= UNROLL:
+            for i in range(count):
+                step(i)
+        else:
+
+            def body(i, carry):
+                step(i)
+                return carry
+
+            lax.fori_loop(0, count, body, 0)
+
+    def other_group(off):
+        return lax.rem(mine_g + off, replicas)
+
+    def other_device(i):
+        return i + jnp.where(i >= me, 1, 0)
+
     def send_group(ref, sem):
-        def step(off, carry):
-            send(ref, ref, sem, {"expert": lax.rem(me + off, n)})
-            return carry
-
-        lax.fori_loop(1, n, step, 0)
-
-    def send_twins(ref, sem):
-        for off in range(1, replicas):
-            send(ref, ref, sem, {"group": lax.rem(mine_g + off, replicas)})
-
-    def send_others(ref, sem):
-        for other in range(1, replicas):
-
-            def step(off, carry, other=other):
-                group = lax.rem(mine_g + other, replicas)
-                send(ref, ref, sem, {"group": group, "expert": lax.rem(me + off, n)})
-                return carry
-
-            lax.fori_loop(0, n, step, 0)
+        loop(n - 1, lambda i: send(ref, ref, sem, {"expert": other_device(i)}))
 
     def await_bytes(ref, sem):
         pltpu.make_async_copy(ref, ref, sem).wait()
 
     attended_piece = attended_all.at[mine, :]
     send_group(attended_piece, 0)
-    send_group(hidden_all.at[mine_g, mine, :], 1)
-    send_twins(routes_all.at[mine_g], 2)
+    send_group(hidden_all.at[mine, :], 1)
+    for off in range(1, replicas):
+        send(routes_all.at[mine_g], routes_all.at[mine_g], 2, {"group": other_group(off)})
+
+    square = (n, n)
+    down_index = lax.broadcasted_iota(jnp.int32, square, 0)
+    across_index = lax.broadcasted_iota(jnp.int32, square, 1)
+
+    def placed(group):
+        across = jnp.broadcast_to(routes_all[group].astype(F32), square)
+        route = jnp.sum(
+            jnp.where(down_index == across_index, across, 0.0), axis=1, keepdims=True
+        )
+        same = jnp.broadcast_to(route, square) == across
+        slot_down = jnp.sum(
+            jnp.where(same & (across_index < down_index), 1.0, 0.0), axis=1, keepdims=True
+        )
+        slot_across = jnp.sum(
+            jnp.where(same & (down_index < across_index), 1.0, 0.0), axis=0, keepdims=True
+        )
+        return route, slot_down, across[0:1, :], slot_across
+
+    route, slot_down, route_across, slot_across = placed(mine_g)
+
+    def picks(expert, slot):
+        wanted = jnp.broadcast_to(route_across, expert.shape) == expert.astype(F32)
+        ranked = jnp.broadcast_to(slot_across, slot.shape) == slot.astype(F32)
+        return jnp.where(wanted & ranked, 1.0, 0.0).astype(BF16)
+
+    def picks_for_device(group):
+        slot = lax.broadcasted_iota(jnp.int32, (served, n), 0)
+        expert = jnp.full((served, n), expert_of(group, me), jnp.int32)
+        return picks(expert, jnp.where(slot < slots, slot, n))
+
+    def picks_for_group(group):
+        row = lax.broadcasted_iota(jnp.int32, (n * slots, n), 0)
+        return picks(expert_of(group, row // slots), row - row // slots * slots)
+
+    own_picks = picks_for_device(mine_g)
+    twin_picks = [picks_for_device(other_group(off)) for off in range(1, replicas)]
+    group_picks = [picks_for_group(other_group(off)) for off in range(1, replicas)]
+    guests_ref[...] = jnp.zeros(guests_ref.shape, F32)
+
+    def unfolded(folded):
+        unfold[...] = folded[...].astype(F32)
+        return [unfold[pl.ds(h, n, stride=HEADS), :].astype(BF16) for h in range(HEADS)]
 
     others = pl.ds(0, (n - 1) * HEADS)
-    token = lax.broadcasted_iota(jnp.int32, (world, 1), 0)
-    await_bytes(hidden_all.at[0, others, :], recv_sem.at[1])
-    send_twins(hidden_all.at[mine_g], 3)
+    twins = pl.ds(0, replicas - 1)
+    w_out_copy.wait()
     await_bytes(attended_all.at[others, :], recv_sem.at[0])
-    unfold[pl.ds(0, n * HEADS), :] = attended_all[...].astype(F32)
-    attended = jnp.concatenate(
-        [unfold[pl.ds(h, n, stride=HEADS), :].astype(BF16) for h in range(HEADS)], axis=1
-    )
-    w_out_copy.wait()
+    attended = jnp.concatenate(unfolded(attended_all), axis=1)
     projected = jnp.dot(attended, w_out[...], preferred_element_type=F32).astype(BF16)
-    cols = projected.shape[1]
     my_cols = pl.ds(pl.multiple_of(me * cols, cols), cols)
     if cols % 128 == 0:
-        projected_all[mine_g, :, my_cols] = projected
-        piece_ref = projected_all.at[mine_g, :, my_cols]
-        near = projected_all.at[0, :, pl.ds(0, (n - 1) * cols)]
+        projected_all[:, my_cols] = projected
+        piece_ref = projected_all.at[:, my_cols]
+        near = projected_all.at[:, pl.ds(0, (n - 1) * cols)]
     else:
-        projected_all[mine_g, me] = projected
-        piece_ref = projected_all.at[mine_g, me]
-        near = projected_all.at[0, pl.ds(0, n - 1)]
-    far = projected_all.at[pl.ds(0, replicas - 1)]
-    send_group(piece_ref, 4)
-    send_others(piece_ref, 5)
-
-    twins = pl.ds(0, replicas - 1)
+        projected_all[me] = projected
+        piece_ref = projected_all.at[me]
+        near = projected_all.at[pl.ds(0, n - 1)]
+    for off in range(1, replicas):
+        picked = jnp.dot(group_picks[off - 1], projected, preferred_element_type=F32)
+        for j in range(n):
+            picked_projected[off - 1, j] = picked[j * slots : (j + 1) * slots, :]
+        group = other_group(off)
+        loop(
+            n,
+            lambda j: send(
+                picked_projected.at[off - 1, j],
+                guest_projected.at[off - 1, me],
+                4,
+                {"group": group, "expert": j},
+            ),
+        )
+    send_group(piece_ref, 3)
+    await_bytes(hidden_all.at[others, :], recv_sem.at[1])
+    every_hidden = jnp.concatenate(unfolded(hidden_all), axis=1)
+    for off in range(1, replicas):
+        picked_hidden[off - 1] = jnp.dot(
+            twin_picks[off - 1], every_hidden, preferred_element_type=F32
+        )[:slots, :]
+        send(
+            picked_hidden.at[off - 1],
+            guest_hidden.at[off - 1],
+            5,
+            {"group": other_group(off)},
+        )
+
     await_bytes(routes_all.at[twins], recv_sem.at[2])
-    square = (n, n)
-    on_diagonal = lax.broadcasted_iota(jnp.int32, square, 0) == lax.broadcasted_iota(
-        jnp.int32, square, 1
-    )
-    chosen_expert = jnp.concatenate(
-        [
-            jnp.sum(
-                jnp.where(on_diagonal, jnp.broadcast_to(routes_all[i].astype(F32), square), 0.0),
-                axis=1,
-                keepdims=True,
-            )
-            for i in range(replicas)
-        ],
-        axis=0,
-    )
+    my_expert = expert_of(mine_g, me).astype(F32)
+
+    def places(their_route, their_slot):
+        here = their_route == my_expert
+        return [jnp.where(here & (their_slot == float(k)), 1.0, 0.0) for k in range(slots)]
+
+    token_places = [places(route, slot_down)]
+    for off in range(1, replicas):
+        their_route, their_slot, _, _ = placed(other_group(replicas - off))
+        token_places.append(places(their_route, their_slot))
     gain_copy.wait()
     router_copy.wait()
-    expert_ids = lax.broadcasted_iota(jnp.int32, (world, EXPERTS), 1).astype(F32)
-    chosen_router = jnp.dot(
-        jnp.where(chosen_expert == expert_ids, 1.0, 0.0).astype(BF16),
-        router[...],
-        preferred_element_type=F32,
+    gain_row = gain[...].astype(F32).reshape(1, width)
+    router_row = jnp.sum(
+        jnp.where(
+            lax.broadcasted_iota(jnp.int32, (EXPERTS, width), 0) == expert_of(mine_g, me),
+            router[...].astype(F32),
+            0.0,
+        ),
+        axis=0,
+        keepdims=True,
     )
-    await_bytes(hidden_all.at[twins], recv_sem.at[3])
-    unfold[...] = hidden_all[...].reshape(world * HEADS, HEAD_DIM).astype(F32)
-    every_hidden = jnp.concatenate(
-        [unfold[pl.ds(h, world, stride=HEADS), :] for h in range(HEADS)], axis=1
-    )
-    await_bytes(near, recv_sem.at[4])
-    await_bytes(far, recv_sem.at[5])
+
+    def norm(residual):
+        centered = residual - jnp.mean(residual, axis=1, keepdims=True)
+        variance = jnp.mean(centered * centered, axis=1, keepdims=True)
+        return centered / jnp.sqrt(jnp.maximum(variance, 0.25)) * gain_row
+
+    token = lax.broadcasted_iota(jnp.int32, (n, 1), 0)
+    shared_up_copy.wait()
+    for chunk in range(up_chunks):
+        up_copy(chunk).wait()
+    await_bytes(near, recv_sem.at[3])
     if cols % 128 == 0:
-        every_projected = projected_all[...].reshape(world, width).astype(F32)
+        every_projected = projected_all[...].astype(F32)
     else:
-        every_projected = jnp.concatenate(
-            [
-                jnp.concatenate([projected_all[i, d].astype(F32) for d in range(n)], axis=1)
-                for i in range(replicas)
-            ],
-            axis=0,
-        )
-    residual = every_hidden + every_projected
-    centered = residual - jnp.mean(residual, axis=1, keepdims=True)
-    variance = jnp.mean(centered * centered, axis=1, keepdims=True)
-    normed = (
-        centered / jnp.sqrt(jnp.maximum(variance, 0.25)) * gain[...].astype(F32).reshape(1, width)
+        every_projected = jnp.concatenate([projected_all[d].astype(F32) for d in range(n)], axis=1)
+    residual = every_hidden.astype(F32) + every_projected
+    normed = norm(residual).astype(BF16)
+    own_served = jnp.dot(own_picks, normed, preferred_element_type=F32)
+    own_ref[...] = jnp.sum(jnp.where(token == me, residual, 0.0), axis=0, keepdims=True)
+    shared_ref[...] = gelu(
+        jnp.dot(normed, shared_up[...], preferred_element_type=F32)
     ).astype(BF16)
-    normed_ref[...] = normed
-    own_ref[...] = jnp.sum(jnp.where(token == rank, residual, 0.0), axis=0, keepdims=True)
-    chosen = jnp.sum(normed.astype(F32) * chosen_router, axis=1, keepdims=True)
+
+    await_bytes(guest_hidden, recv_sem.at[5])
+    await_bytes(guest_projected, recv_sem.at[4])
+    for off in range(1, replicas):
+        theirs = jnp.concatenate([guest_projected[off - 1, d] for d in range(n)], axis=1)
+        guests_ref[pl.ds(off * slots, slots), :] = norm(guest_hidden[off - 1] + theirs)
+    everyone = (own_served + guests_ref[...]).astype(BF16)
+    normed_ref[...] = everyone
+    chosen = jnp.sum(everyone.astype(F32) * router_row, axis=1, keepdims=True)
     gate_ref[...] = 1.0 / (1.0 + jnp.exp(-chosen))
-
-    shared_up_copy.wait()
-    shared_act = gelu(jnp.dot(normed_ref[...], shared_up[...], preferred_element_type=F32))
-    if shared_share == shared_units:
-        unit = lax.broadcasted_iota(jnp.int32, shared_act.shape, 1)
-        shared_act = jnp.where(unit // (shared_units // replicas) == mine_g, shared_act, 0.0)
-    shared_ref[...] = shared_act.astype(BF16)
-
-    together = math.gcd(TOGETHER, up_chunks)
-
-    def up_step(step, carry):
-        chunks = [step * together + i for i in range(together)]
-        for chunk in chunks:
-            up_copy(chunk).wait()
-        for chunk in chunks:
-            act = gelu(jnp.dot(normed_ref[...], up[chunk], preferred_element_type=F32))
-            expert = (me * units + mine_g * share + chunk * chunk_cols) // FF
-            inner[:, pl.ds(pl.multiple_of(chunk * chunk_cols, chunk_cols), chunk_cols)] = jnp.where(
-                chosen_expert == expert.astype(F32), act, 0.0
-            ).astype(BF16)
-        return carry
-
-    lax.fori_loop(0, up_chunks // together, up_step, 0)
-    shared_down_copy.wait()
+    for chunk in range(up_chunks):
+        act = gelu(jnp.dot(normed_ref[...], up[chunk], preferred_element_type=F32))
+        inner[:, pl.ds(chunk * chunk_cols, chunk_cols)] = act.astype(BF16)
 
     group_rows = GROUP_COLS // 128
     groups = width // GROUP_COLS
     blocks_per_group = blocks // groups
+    shared_down_copy.wait()
 
     for group in range(groups):
+        half = blocks_per_group * pieces
+        for copy in chunk_copies[up_chunks + 1 + group * half : up_chunks + 1 + (group + 1) * half]:
+            copy.wait()
         for index in range(blocks_per_group):
             block = group * blocks_per_group + index
-            for part in range(pieces):
-                down_copy(block, part).wait()
-            acc = jnp.dot(inner[...], down[block], preferred_element_type=F32)
-            shared = jnp.dot(
-                shared_ref[...],
-                shared_down[:, pl.ds(block * block_cols, block_cols)],
-                preferred_element_type=F32,
-            )
-            terms = shared + gate_ref[...] * acc
-            for k in range(block_cols // 128):
-                row = index * (block_cols // 128) + k
-                terms_buf[pl.ds(row, world, stride=group_rows), :] = terms[:, k * 128 : (k + 1) * 128]
+            acc = gate_ref[...] * jnp.dot(inner[...], down[block], preferred_element_type=F32)
+            terms = []
+            for side in range(replicas):
+                if side == 0:
+                    total = jnp.dot(
+                        shared_ref[...],
+                        shared_down[:, pl.ds(block * block_cols, block_cols)],
+                        preferred_element_type=F32,
+                    )
+                else:
+                    total = jnp.zeros((n, block_cols), F32)
+                for k in range(slots):
+                    row = side * slots + k
+                    total = total + token_places[side][k] * acc[row : row + 1, :]
+                terms.append(total)
+            for side in range(replicas):
+                for k in range(block_cols // 128):
+                    row = side * n * group_rows + index * (block_cols // 128) + k
+                    terms_buf[pl.ds(row, n, stride=group_rows), :] = terms[side][
+                        :, k * 128 : (k + 1) * 128
+                    ]
         send_buf[group] = terms_buf[...].reshape(world, group_rows, 128).astype(BF16)
 
-        def send_terms(off, carry, group=group):
-            peer = lax.rem(rank + off, world)
-            send(send_buf.at[group, peer], recv_buf.at[group, rank], 6 + group, place(peer))
-            return carry
-
-        lax.fori_loop(1, world, send_terms, 0)
-        recv_buf[group, rank] = send_buf[group, rank]
+        def send_terms(i, group=group):
+            def to(side, device):
+                where = side * n
+                send(
+                    send_buf.at[group, where + device],
+                    recv_buf.at[group, where + me],
+                    6 + group,
+                    {"group": other_group(replicas - side), "expert": device},
+                )
+
+            for side in range(1, replicas):
+                to(side, i)
+            if isinstance(i, int):
+                if i < n - 1:
+                    to(0, other_device(i))
+            else:
+
+                @pl.when(i < n - 1)
+                def _():
+                    to(0, other_device(i))
+
+        loop(n, send_terms)
+        recv_buf[group, me] = send_buf[group, me]
 
     for group in range(groups):
         landed = recv_buf.at[group, pl.ds(0, world - 1)]
@@ -421,11 +497,11 @@
             out_ref[:, where] = (own_ref[:, where] + summed[j : j + 1, :]).astype(out_ref.dtype)
 
     await_bytes(attended_all.at[others, :], send_sem.at[0])
-    await_bytes(hidden_all.at[0, others, :], send_sem.at[1])
+    await_bytes(hidden_all.at[others, :], send_sem.at[1])
     await_bytes(routes_all.at[twins], send_sem.at[2])
-    await_bytes(hidden_all.at[twins], send_sem.at[3])
-    await_bytes(near, send_sem.at[4])
-    await_bytes(far, send_sem.at[5])
+    await_bytes(near, send_sem.at[3])
+    await_bytes(guest_projected, send_sem.at[4])
+    await_bytes(guest_hidden, send_sem.at[5])
     for group in range(groups):
         sent = send_buf.at[group, pl.ds(0, world - 1)]
         await_bytes(sent, send_sem.at[6 + group])
@@ -457,17 +533,17 @@
         width = query.shape[1]
         share = expert_up.shape[1] // replicas
         cache = key_cache.shape[1]
-        shared_share = shared_up.shape[1] // replicas
-        if shared_share % 128:
-            shared_share = shared_up.shape[1]
+        shared_units = shared_up.shape[1]
         cols = w_out.shape[1]
+        slots = max(1, n // MOST_ROUTED)
+        served = -(-slots * replicas // 16) * 16
         chunk_cols = min(CHUNK, share)
         up_chunks = share // chunk_cols
         blocks = width // BLOCK
         pieces = share // min(share, width)
         groups = width // GROUP_COLS
         rows_sent = GROUP_COLS // 128
-        gathered = (replicas, n, width) if cols % 128 == 0 else (replicas, n, n, cols)
+        gathered = (n, width) if cols % 128 == 0 else (n, n, cols)
         vmem = pltpu.VMEM
         hbm = pl.BlockSpec(memory_space=pl.ANY)
         return pl.pallas_call(
@@ -487,18 +563,23 @@
                 vmem((cache, width), BF16),
                 vmem((width, cols), BF16),
                 vmem((EXPERTS, width), BF16),
-                vmem((width, shared_share), BF16),
-                vmem((shared_share, width), BF16),
+                vmem((width, shared_units), BF16),
+                vmem((shared_units, width), BF16),
                 vmem((up_chunks, width, chunk_cols), BF16),
                 vmem((blocks, share, BLOCK), BF16),
                 vmem((n * HEADS, HEAD_DIM), BF16),
-                vmem((replicas, n * HEADS, HEAD_DIM), BF16),
-                vmem((world * HEADS, HEAD_DIM), F32),
+                vmem((n * HEADS, HEAD_DIM), BF16),
+                vmem((n * HEADS, HEAD_DIM), F32),
                 vmem(gathered, BF16),
-                vmem((world, share), BF16),
-                vmem((world, width), BF16),
-                vmem((world, 1), F32),
-                vmem((world, shared_share), BF16),
+                vmem((replicas - 1, slots, width), F32),
+                vmem((replicas - 1, slots, width), F32),
+                vmem((replicas - 1, n, slots, cols), F32),
+                vmem((replicas - 1, n, slots, cols), F32),
+                vmem((served, width), F32),
+                vmem((served, share), BF16),
+                vmem((served, width), BF16),
+                vmem((served, 1), F32),
+                vmem((n, shared_units), BF16),
                 vmem((1, width), F32),
                 vmem((world * rows_sent, 128), F32),
                 vmem((groups, world, rows_sent, 128), BF16),

time: 31.9 us -> 28.5 us (0.89)
  Pallas kernels: 30.4 us -> 27.1 us
    pallas_call x1, Pallas kernels: 30.4 us -> 27.1 us  [body(): pl.pallas_call(functools.partial(kernel, replicas, n), out_shape=pltpu.VM...]
where the time goes in v2:
time: 28.5 us; the launch traced here: 28.3 us
  Pallas kernels  27.1 us (95%)
  between operations  0.66 us (2%)
  local copies, waits for them, and re-layouts  0.6 us (2%)
    pallas_call x1, Pallas kernels, body(): pl.pallas_call(functools.partial(kernel, replicas, n), out_shape=pltpu.VM...  27.1 us
    unnamed x1, local copies, waits for them, and re-layouts  0.6 us

profile of v2, /device:TPU:0, one launch (start us, length us, event | category | flops | bytes accessed | tf_op | source)
XLA Modules:
  0.0 28.3 jit_solution(15600842987202759391)
XLA Ops:
  0.7 27.1 %shard_map.145 = bf16[1,2048]{1,0:T(2,128)(2,1)S(1)} custom-call(s32[1]{0:T(128)S(6)} %copy.18.lengths_hbm, s32[1,16]{1,0:T(1,128)} %bitcast.7, bf16[1,2048]{1,0:T(2,128)(2,1)} %query_hbm.1, bf16[1,2048]{1,0:T(2,128)(2,1)} %key_new_hbm.1, bf16[1,2048]{1,0:T(2,128)(2,1)} %value_new_hbm.1, bf16[1,2048]{1,0:T(2,128)(2,1)} %hidden_hbm.1, ...), custom_call_target="tpu_custom_call" | custom-call | tf_op jit(solution)/shard_map/pallas_call | solution.py:549
  27.7 0.6 %copy.17 = bf16[1,2048]{1,0:T(2,128)(2,1)} copy(bf16[1,2048]{1,0:T(2,128)(2,1)S(1)} %shard_map.145) | data formatting | bytes 8192

commit v3 on v2

--- a/solution.py
+++ b/solution.py
@@ -14,11 +14,11 @@
 EXPERTS = 32
 CHUNK = 512
 BLOCK = 512
-EARLY = 3
+EARLY = 99
 PRIORITY = 1
 UNROLL = 32
 MOST_ROUTED = 8
-GROUP_COLS = 1024
+GROUP_COLS = 2048
 MESH = pl.DeviceIdType.MESH
 F32 = jnp.float32
 BF16 = jnp.bfloat16
@@ -173,7 +173,7 @@
             chunk_copies[issued].start(priority=PRIORITY)
             issued += 1
 
-    for copy in (query_copy, key_new_copy, keys_copy, values_copy, value_new_copy, hidden_copy, lengths_copy, routes_copy, w_out_copy):
+    for copy in (query_copy, key_new_copy, keys_copy, values_copy, value_new_copy, hidden_copy, lengths_copy, routes_copy, w_out_copy, gain_copy, router_copy, shared_up_copy):
         copy.start()
     start_chunks(EARLY)
 
@@ -224,8 +224,6 @@
     lengths_copy.wait()
     values_copy.wait()
     value_new_copy.wait()
-    for copy in (gain_copy, router_copy, shared_up_copy):
-        copy.start()
     start_chunks(len(chunk_copies))
 
     position = lax.broadcasted_iota(jnp.int32, scores.shape, 1)

time: 28.5 us -> 28 us (0.982)
  Pallas kernels: 27.1 us -> 26.5 us
    pallas_call x1, Pallas kernels: 27.1 us -> 26.5 us  [body(): pl.pallas_call(functools.partial(kernel, replicas, n), out_shape=pltpu.VM...]
where the time goes in v3:
time: 28 us; the launch traced here: 27.8 us
  Pallas kernels  26.5 us (95%)
  between operations  0.66 us (2%)
  local copies, waits for them, and re-layouts  0.6 us (2%)
    pallas_call x1, Pallas kernels, body(): pl.pallas_call(functools.partial(kernel, replicas, n), out_shape=pltpu.VM...  26.5 us
    unnamed x1, local copies, waits for them, and re-layouts  0.6 us

profile of v3, /device:TPU:0, one launch (start us, length us, event | category | flops | bytes accessed | tf_op | source)
XLA Modules:
  0.0 27.8 jit_solution(7105503434929443411)
XLA Ops:
  0.7 26.5 %shard_map.145 = bf16[1,2048]{1,0:T(2,128)(2,1)S(1)} custom-call(s32[1]{0:T(128)S(6)} %copy.18.lengths_hbm, s32[1,16]{1,0:T(1,128)} %bitcast.7, bf16[1,2048]{1,0:T(2,128)(2,1)} %query_hbm.1, bf16[1,2048]{1,0:T(2,128)(2,1)} %key_new_hbm.1, bf16[1,2048]{1,0:T(2,128)(2,1)} %value_new_hbm.1, bf16[1,2048]{1,0:T(2,128)(2,1)} %hidden_hbm.1, ...), custom_call_target="tpu_custom_call" | custom-call | tf_op jit(solution)/shard_map/pallas_call | solution.py:547
  27.2 0.6 %copy.17 = bf16[1,2048]{1,0:T(2,128)(2,1)} copy(bf16[1,2048]{1,0:T(2,128)(2,1)S(1)} %shard_map.145) | data formatting | bytes 8192

commit v4 on v3

--- a/solution.py
+++ b/solution.py
@@ -84,6 +84,7 @@
     down_sem,
     send_sem,
     recv_sem,
+    ready_sem,
 ):
     mine_g = lax.axis_index("group")
     me = lax.axis_index("expert")
@@ -177,16 +178,30 @@
         copy.start()
     start_chunks(EARLY)
 
-    def place(peer):
-        return {"group": peer // n, "expert": lax.rem(peer, n)}
-
-    def greet(off, carry):
-        pl.semaphore_signal(
-            barrier, inc=1, device_id=place(lax.rem(rank + off, world)), device_id_type=MESH
-        )
-        return carry
-
-    lax.fori_loop(1, world, greet, 0)
+    def loop(count, step):
+        if count <= UNROLL:
+            for i in range(count):
+                step(i)
+        else:
+
+            def body(i, carry):
+                step(i)
+                return carry
+
+            lax.fori_loop(0, count, body, 0)
+
+    def other_group(off):
+        return lax.rem(mine_g + off, replicas)
+
+    def other_device(i):
+        return i + jnp.where(i >= me, 1, 0)
+
+    def greet(to):
+        pl.semaphore_signal(barrier, inc=1, device_id=to, device_id_type=MESH)
+
+    loop(n - 1, lambda i: greet({"expert": other_device(i)}))
+    for off in range(1, replicas):
+        greet({"group": other_group(off)})
 
     rows = lax.broadcasted_iota(jnp.int32, (HEADS, width), 0)
     lanes = lax.broadcasted_iota(jnp.int32, (HEADS, width), 1)
@@ -239,7 +254,7 @@
     attended_all[mine, :] = fold(mixed).astype(BF16)
     routes_copy.wait()
 
-    pl.semaphore_wait(barrier, world - 1)
+    pl.semaphore_wait(barrier, n - 1 + replicas - 1)
 
     def send(src, dst, sem, to):
         pltpu.make_async_remote_copy(
@@ -251,24 +266,6 @@
             device_id_type=MESH,
         ).start()
 
-    def loop(count, step):
-        if count <= UNROLL:
-            for i in range(count):
-                step(i)
-        else:
-
-            def body(i, carry):
-                step(i)
-                return carry
-
-            lax.fori_loop(0, count, body, 0)
-
-    def other_group(off):
-        return lax.rem(mine_g + off, replicas)
-
-    def other_device(i):
-        return i + jnp.where(i >= me, 1, 0)
-
     def send_group(ref, sem):
         loop(n - 1, lambda i: send(ref, ref, sem, {"expert": other_device(i)}))
 
@@ -280,6 +277,11 @@
     send_group(hidden_all.at[mine, :], 1)
     for off in range(1, replicas):
         send(routes_all.at[mine_g], routes_all.at[mine_g], 2, {"group": other_group(off)})
+
+    for off in range(1, replicas):
+        pl.semaphore_signal(
+            ready_sem, inc=1, device_id={"group": other_group(off)}, device_id_type=MESH
+        )
 
     square = (n, n)
     down_index = lax.broadcasted_iota(jnp.int32, square, 0)
@@ -344,6 +346,8 @@
         for j in range(n):
             picked_projected[off - 1, j] = picked[j * slots : (j + 1) * slots, :]
         group = other_group(off)
+        if off == 1:
+            pl.semaphore_wait(ready_sem, replicas - 1)
         loop(
             n,
             lambda j: send(
@@ -432,11 +436,12 @@
     shared_down_copy.wait()
 
     for group in range(groups):
-        half = blocks_per_group * pieces
-        for copy in chunk_copies[up_chunks + 1 + group * half : up_chunks + 1 + (group + 1) * half]:
-            copy.wait()
         for index in range(blocks_per_group):
             block = group * blocks_per_group + index
+            if block % 2 == 0:
+                for later in range(block, min(block + 2, blocks)):
+                    for part in range(pieces):
+                        down_copy(later, part).wait()
             acc = gate_ref[...] * jnp.dot(inner[...], down[block], preferred_element_type=F32)
             terms = []
             for side in range(replicas):
@@ -587,6 +592,7 @@
                 pltpu.SemaphoreType.DMA((blocks * pieces,)),
                 pltpu.SemaphoreType.DMA((6 + groups,)),
                 pltpu.SemaphoreType.DMA((6 + groups,)),
+                pltpu.SemaphoreType.REGULAR,
             ],
             compiler_params=pltpu.CompilerParams(
                 collective_id=0, has_side_effects=True, vmem_limit_bytes=66_900_000

time: 28 us -> 28.1 us (level)
  no operation moved by 1% of the time
where the time goes in v4:
time: 28.1 us; the launch traced here: 27.9 us
  Pallas kernels  26.7 us (95%)
  between operations  0.66 us (2%)
  local copies, waits for them, and re-layouts  0.6 us (2%)
    pallas_call x1, Pallas kernels, body(): pl.pallas_call(functools.partial(kernel, replicas, n), out_shape=pltpu.VM...  26.7 us
    unnamed x1, local copies, waits for them, and re-layouts  0.6 us

profile of v4, /device:TPU:0, one launch (start us, length us, event | category | flops | bytes accessed | tf_op | source)
XLA Modules:
  0.0 27.9 jit_solution(13194556415281478004)
XLA Ops:
  0.7 26.7 %shard_map.145 = bf16[1,2048]{1,0:T(2,128)(2,1)S(1)} custom-call(s32[1]{0:T(128)S(6)} %copy.18.lengths_hbm, s32[1,16]{1,0:T(1,128)} %bitcast.7, bf16[1,2048]{1,0:T(2,128)(2,1)} %query_hbm.1, bf16[1,2048]{1,0:T(2,128)(2,1)} %key_new_hbm.1, bf16[1,2048]{1,0:T(2,128)(2,1)} %value_new_hbm.1, bf16[1,2048]{1,0:T(2,128)(2,1)} %hidden_hbm.1, ...), custom_call_target="tpu_custom_call" | custom-call | tf_op jit(solution)/shard_map/pallas_call | solution.py:552
  27.3 0.6 %copy.17 = bf16[1,2048]{1,0:T(2,128)(2,1)} copy(bf16[1,2048]{1,0:T(2,128)(2,1)S(1)} %shard_map.145) | data formatting | bytes 8192
